TPU v7x, 32 devices: a whole 2x2x4 slice. The times are simulated.
32 devices in a mesh: px: 8 (over z, y), py: 4 (over x, core).
Axes of the slice: x: 2, y: 2, z: 4, core: 2. Of those that a mesh axis runs over, the one named last changes fastest.
Arguments:
- initial_field: float32 [1, 2048, 2048], P(None, ('px', 'py')), may hold values from -6 to 6
- target_field: float32 [1, 2048, 2048], P(None, ('px', 'py')), may hold values from -6 to 6
- forcing: float32 [2, 2048, 2048], P(None, ('px', 'py')), may hold values from -6 to 6
Outputs:
- next_field: float32 [1, 2048, 2048], P(None, ('px', 'py'))
- objective: float32 [], replicated
- field_grad: float32 [1, 2048, 2048], P(None, ('px', 'py'))
- forcing_grad: float32 [2, 2048, 2048], P(None, ('px', 'py'))
All inputs are finite; a program needn't handle non-finite values.
Results may differ from a plain program's by a relative error of at most 0.00014.
Values sent between devices are 32-bit elements; how exact they have to be, the bound alone decides.
A program may use at most 128 MiB of HBM per device.

v0:
```python
import math
import jax
import jax.numpy as jnp
from jax import lax
from jax.sharding import PartitionSpec as P

time_step = 0.25
highest = lax.Precision.HIGHEST


def factor_pair(length):
    first_len = int(math.isqrt(length))
    while length % first_len:
        first_len -= 1
    return (first_len, length // first_len)


def phases(row_count, col_count, period, sign_value, factor):
    product = (
        jnp.arange(row_count, dtype=jnp.int32)[:, None]
        * jnp.arange(col_count, dtype=jnp.int32)[None, :]
        % period
    )
    angles = product.astype(jnp.float32) * (2.0 * math.pi / period)
    return (factor * jnp.cos(angles), sign_value * factor * jnp.sin(angles))


def complex_einsum(formula, left_real, left_imag, table_pair):
    real_term = jnp.einsum(formula, left_real, table_pair[0], precision=highest)
    imag_term = jnp.einsum(formula, left_real, table_pair[1], precision=highest)
    if left_imag is None:
        return (real_term, imag_term)
    real_term = real_term - jnp.einsum(formula, left_imag, table_pair[1], precision=highest)
    imag_term = imag_term + jnp.einsum(formula, left_imag, table_pair[0], precision=highest)
    return (real_term, imag_term)


def transform(real_part, imag_part, sign_value, leading, real_only):
    if leading:
        members, length, span_rows = real_part.shape
        first_len, second_len = factor_pair(length)
        new_shape = (members, first_len, second_len, span_rows)
        formula = "mabr,ak->mrkb"
    else:
        members, span_rows, length = real_part.shape
        first_len, second_len = factor_pair(length)
        new_shape = (members, span_rows, first_len, second_len)
        formula = "mrab,ak->mrkb"
    shaped_real = real_part.reshape(new_shape)
    shaped_imag = None if imag_part is None else imag_part.reshape(new_shape)
    sectioned_out = complex_einsum(
        formula, shaped_real, shaped_imag, phases(first_len, first_len, first_len, sign_value, 1.0)
    )
    twiddle = phases(first_len, second_len, length, sign_value, 1.0 / math.sqrt(length))
    turned_real = sectioned_out[0] * twiddle[0] - sectioned_out[1] * twiddle[1]
    turned_imag = sectioned_out[0] * twiddle[1] + sectioned_out[1] * twiddle[0]
    last_table = phases(second_len, second_len, second_len, sign_value, 1.0)
    final_formula = "mrkb,bq->mrqk"
    if real_only:
        out_real = jnp.einsum(final_formula, turned_real, last_table[0], precision=highest)
        out_real = out_real - jnp.einsum(
            final_formula, turned_imag, last_table[1], precision=highest
        )
        return (out_real.reshape(members, span_rows, length), None)
    out_real, out_imag = complex_einsum(final_formula, turned_real, turned_imag, last_table)
    return (
        out_real.reshape(members, span_rows, length),
        out_imag.reshape(members, span_rows, length),
    )


def regroup(real_part, imag_part):
    moved_real, moved_imag = (
        lax.all_to_all(real_part, ("px", "py"), split_axis=2, concat_axis=1, tiled=True),
        lax.all_to_all(imag_part, ("px", "py"), split_axis=2, concat_axis=1, tiled=True),
    )
    return (moved_real, moved_imag)


def spectral(real_part, imag_part):
    first_pass = transform(real_part, imag_part, -1.0, False, False)
    moved = regroup(first_pass[0], first_pass[1])
    return transform(moved[0], moved[1], -1.0, True, False)


def physical(real_part, imag_part, real_only):
    first_pass = transform(real_part, imag_part, 1.0, False, False)
    moved = regroup(first_pass[0], first_pass[1])
    return transform(moved[0], moved[1], 1.0, True, real_only)


def waves_of(position, count):
    signed = jnp.where(position < count // 2, position, position - count)
    waves = 4.0 * signed.astype(jnp.float32) / count
    derive = jnp.where(position == count // 2, jnp.float32(0.0), waves)
    return (waves, derive)


def per_device(initial_field, target_field, forcing):
    members = initial_field.shape[0]
    full_second = initial_field.shape[2]
    spec_rows = forcing.shape[1]
    full_first = forcing.shape[2]
    device = lax.axis_index(("px", "py"))
    position_first = jnp.arange(full_first, dtype=jnp.int32)
    position_second = device * spec_rows + jnp.arange(spec_rows, dtype=jnp.int32)
    wave_first, deriv_first = waves_of(position_first, full_first)
    wave_second, deriv_second = waves_of(position_second, full_second)
    wave_first = wave_first[None, :]
    deriv_first = deriv_first[None, :]
    wave_second = wave_second[:, None]
    deriv_second = deriv_second[:, None]
    wave_square = wave_first * wave_first + wave_second * wave_second
    denominator = 1.0 + time_step * (wave_square * wave_square - wave_square)
    state_real, state_imag = spectral(initial_field, None)
    slope_real = -deriv_first * state_imag - deriv_second * state_real
    slope_imag = deriv_first * state_real - deriv_second * state_imag
    grad_first, grad_second = physical(slope_real, slope_imag, False)
    nonlinear = -0.5 * (grad_first * grad_first + grad_second * grad_second)
    nonlinear_real, nonlinear_imag = spectral(nonlinear, None)
    next_real = (state_real + time_step * (nonlinear_real + forcing[0])) / denominator
    next_imag = (state_imag + time_step * (nonlinear_imag + forcing[1])) / denominator
    next_field, unused_part = physical(next_real, next_imag, True)
    residual = next_field - target_field
    total = lax.psum(0.5 * jnp.sum(residual * residual), ("px", "py"))
    objective = total / (members * full_first * full_second)
    misfit_real, misfit_imag = spectral(residual, None)
    coef_real = misfit_real / denominator
    coef_imag = misfit_imag / denominator
    forcing_grad = time_step * jnp.stack([jnp.sum(coef_real, axis=0), jnp.sum(coef_imag, axis=0)])
    multiplier, unused_other = physical(time_step * coef_real, time_step * coef_imag, True)
    joint_real, joint_imag = spectral(multiplier * grad_first, multiplier * grad_second)
    total_real = coef_real - deriv_first * joint_imag + deriv_second * joint_real
    total_imag = coef_imag + deriv_first * joint_real + deriv_second * joint_imag
    field_grad, unused_last = physical(total_real, total_imag, True)
    return (next_field, objective, field_grad, forcing_grad)


def solution(mesh):
    return jax.shard_map(
        per_device,
        mesh=mesh,
        in_specs=(
            P(None, ("px", "py"), None),
            P(None, ("px", "py"), None),
            P(None, ("px", "py"), None),
        ),
        out_specs=(
            P(None, ("px", "py"), None),
            P(),
            P(None, ("px", "py"), None),
            P(None, ("px", "py"), None),
        ),
        check_vma=False,
    )
```

profile of v0, /device:TPU:0, one launch (start us, length us, event | category | flops | bytes accessed | tf_op | source)
XLA Modules:
  0.0 883.1 jit_solution(13582286991271843873)
XLA Ops:
  13.7 10.5 %reduce = f32[2048,64]{1,0:T(8,128)S(1)} reduce(f32[2048,1,64]{2,1,0:T(1,128)} %bitcast.931, f32[]{:T(128)} %broadcast.1623), dimensions={1}, to_apply=%bitcast.761.reduce_sub_computation | reduce | bytes 1048580
  25.6 7.3 all-to-all-start
  36.5 3.5 fusion.50
  40.6 9.3 %reduce.2 = f32[2048,64]{1,0:T(8,128)S(1)} reduce(f32[2048,1,64]{2,1,0:T(1,128)S(1)} %bitcast.932, f32[]{:T(128)} %broadcast.1623), dimensions={1}, to_apply=%bitcast.763.reduce_sub_computation | reduce | bytes 1048580
  51.3 6.2 all-to-all-start.1
  65.1 8.1 all-to-all-done.1
  81.8 4.2 fusion.236
  118.7 3.5 fusion.43
  123.8 11.5 %reduce.4 = f32[2048,64]{1,0:T(8,128)} reduce(f32[2048,1,64]{2,1,0:T(1,128)} %bitcast.933, f32[]{:T(128)} %broadcast.1623), dimensions={1}, to_apply=%bitcast.765.reduce_sub_computation | reduce | bytes 1048580
  141.4 4.7 fusion.159
  146.1 3.5 fusion.42
  151.2 10.3 %reduce.6 = f32[2048,64]{1,0:T(8,128)S(1)} reduce(f32[2048,1,64]{2,1,0:T(1,128)} %bitcast.934, f32[]{:T(128)} %broadcast.1623), dimensions={1}, to_apply=%bitcast.767.reduce_sub_computation | reduce | bytes 1048580
  162.9 6.3 all-to-all-start.3
  180.8 4.1 all-to-all-done.3
  199.3 4.2 fusion.231
  203.5 4.2 fusion.181
  209.5 4.5 convolution_subtract_fusion.22
  225.7 3.7 fusion.155
  234.5 11.3 %reduce.8 = f32[2048,64]{1,0:T(8,128)} reduce(f32[2048,1,64]{2,1,0:T(1,128)} %bitcast.935, f32[]{:T(128)} %broadcast.1623), dimensions={1}, to_apply=%bitcast.769.reduce_sub_computation | reduce | bytes 1048580
  248.5 3.7 all-to-all-start.4
  252.2 4.7 fusion.153
  262.0 10.3 %reduce.10 = f32[2048,64]{1,0:T(8,128)S(1)} reduce(f32[2048,1,64]{2,1,0:T(1,128)} %bitcast.936, f32[]{:T(128)} %broadcast.1623), dimensions={1}, to_apply=%bitcast.771.reduce_sub_computation | reduce | bytes 1048580
  273.8 6.3 all-to-all-start.5
  310.4 4.2 fusion.226
  314.6 4.2 fusion.196
  320.5 4.5 fusion.35
  344.8 3.5 fusion.31
  349.9 10.3 %reduce.12 = f32[2048,64]{1,0:T(8,128)S(1)} reduce(f32[2048,1,64]{2,1,0:T(1,128)} %bitcast.937, f32[]{:T(128)} %broadcast.1623), dimensions={1}, to_apply=%bitcast.773.reduce_sub_computation | reduce | bytes 1048580
  361.6 6.3 all-to-all-start.6
  371.4 3.5 fusion.30
  375.6 9.3 %reduce.14 = f32[2048,64]{1,0:T(8,128)S(1)} reduce(f32[2048,1,64]{2,1,0:T(1,128)S(1)} %bitcast.938, f32[]{:T(128)} %broadcast.1623), dimensions={1}, to_apply=%bitcast.775.reduce_sub_computation | reduce | bytes 1048580
  386.3 6.2 all-to-all-start.7
  401.2 6.8 all-to-all-done.7
  436.4 10.3 %reduce.16 = f32[2048,64]{1,0:T(8,128)S(1)} reduce(f32[2048,1,64]{2,1,0:T(1,128)} %bitcast.939, f32[]{:T(128)} %broadcast.1623), dimensions={1}, to_apply=%bitcast.777.reduce_sub_computation | reduce | bytes 1048580
  458.7 9.3 %reduce.18 = f32[2048,64]{1,0:T(8,128)S(1)} reduce(f32[2048,1,64]{2,1,0:T(1,128)S(1)} %bitcast.940, f32[]{:T(128)} %broadcast.1623), dimensions={1}, to_apply=%bitcast.779.reduce_sub_computation | reduce | bytes 1048580
  469.4 6.2 all-to-all-start.9
  483.0 8.3 all-to-all-done.9
  499.9 4.2 fusion.218
  536.9 3.5 fusion.18
  542.0 11.3 %reduce.20 = f32[2048,64]{1,0:T(8,128)} reduce(f32[2048,1,64]{2,1,0:T(1,128)} %bitcast.941, f32[]{:T(128)} %broadcast.1623), dimensions={1}, to_apply=%bitcast.781.reduce_sub_computation | reduce | bytes 1048580
  559.5 4.7 fusion.135
  564.2 3.5 fusion.17
  569.3 10.3 %reduce.22 = f32[2048,64]{1,0:T(8,128)S(1)} reduce(f32[2048,1,64]{2,1,0:T(1,128)} %bitcast.942, f32[]{:T(128)} %broadcast.1623), dimensions={1}, to_apply=%bitcast.783.reduce_sub_computation | reduce | bytes 1048580
  581.0 6.3 all-to-all-start.11
  598.8 3.9 all-to-all-done.11
  636.6 3.7 fusion.131
  645.4 11.3 %reduce.24 = f32[2048,64]{1,0:T(8,128)} reduce(f32[2048,1,64]{2,1,0:T(1,128)} %bitcast.943, f32[]{:T(128)} %broadcast.1623), dimensions={1}, to_apply=%bitcast.785.reduce_sub_computation | reduce | bytes 1048580
  659.4 3.5 all-to-all-start.12
  663.0 4.7 fusion.129
  667.7 3.5 fusion.11
  672.8 10.3 %reduce.26 = f32[2048,64]{1,0:T(8,128)S(1)} reduce(f32[2048,1,64]{2,1,0:T(1,128)} %bitcast.944, f32[]{:T(128)} %broadcast.1623), dimensions={1}, to_apply=%bitcast.787.reduce_sub_computation | reduce | bytes 1048580
  684.5 6.5 all-to-all-start.13
  702.6 4.1 all-to-all-done.13
  721.1 4.2 fusion.209
  725.2 4.2 fusion.187
  731.2 4.5 fusion.7
  760.5 3.5 fusion.4
  765.7 11.5 %reduce.28 = f32[2048,64]{1,0:T(8,128)} reduce(f32[2048,1,64]{2,1,0:T(1,128)} %bitcast.945, f32[]{:T(128)} %broadcast.1623), dimensions={1}, to_apply=%bitcast.789.reduce_sub_computation | reduce | bytes 1048580
  783.8 40.5 %psum.7 = f32[]{:T(128)} all-reduce(f32[]{:T(128)S(6)} %mul_shard_map.3), channel_id=1, replica_groups=mesh['px'=8,'py'=4] {'px','py'}, use_global_device_ids=true, to_apply=%region_1.2 | all-reduce | flops 1 | bytes 8 | tf_op jit(solution)/shard_map/psum | solution.py:125
  827.3 4.7 fusion.123
  832.0 3.5 fusion.3
  837.1 10.3 %reduce.30 = f32[2048,64]{1,0:T(8,128)S(1)} reduce(f32[2048,1,64]{2,1,0:T(1,128)} %bitcast.946, f32[]{:T(128)} %broadcast.1623), dimensions={1}, to_apply=%bitcast.791.reduce_sub_computation | reduce | bytes 1048580
  848.9 5.0 all-to-all-start.15
  864.4 5.0 all-to-all-done.15
  (318 shorter events, 447.1 us)
Async XLA Ops:
  25.6 25.7 %all-to-all-start = ((f32[32,1,4096]{2,1,0:T(1,128)}), f32[32,1,4096]{2,1,0:T(1,128)S(1)}, u32[]{:S(2)}, u32[]{:S(2)}) async-start(f32[32,1,4096]{2,1,0:T(1,128)} %reshape.1269), calls=%async_computation | async-start | bytes 1048576 | tf_op jit(solution)/shard_map/all_to_all | solution.py:74
  51.3 21.9 %all-to-all-start.1 = ((f32[32,1,4096]{2,1,0:T(1,128)}), f32[32,1,4096]{2,1,0:T(1,128)S(1)}, u32[]{:S(2)}, u32[]{:S(2)}) async-start(f32[32,1,4096]{2,1,0:T(1,128)} %reshape.1271), calls=%async_computation.1 | async-start | bytes 1048576 | tf_op jit(solution)/shard_map/all_to_all | solution.py:75
  77.3 1.2 copy-start.30
  89.2 1.9 copy-start.25
  109.2 1.0 copy-start.2
  110.2 2.4 copy-start.19
  115.2 7.1 copy-start.10
  138.0 24.9 %all-to-all-start.2 = ((f32[32,1,4096]{2,1,0:T(1,128)}), f32[32,1,4096]{2,1,0:T(1,128)}, u32[]{:S(2)}, u32[]{:S(2)}) async-start(f32[32,1,4096]{2,1,0:T(1,128)} %reshape.1273), calls=%async_computation.2 | async-start | bytes 1048576 | tf_op jit(solution)/shard_map/all_to_all | solution.py:74
  162.9 21.9 %all-to-all-start.3 = ((f32[32,1,4096]{2,1,0:T(1,128)}), f32[32,1,4096]{2,1,0:T(1,128)}, u32[]{:S(2)}, u32[]{:S(2)}) async-start(f32[32,1,4096]{2,1,0:T(1,128)} %reshape.1275), calls=%async_computation.3 | async-start | bytes 1048576 | tf_op jit(solution)/shard_map/all_to_all | solution.py:75
  192.2 2.4 copy-start.31
  209.5 4.5 copy-start.24
  214.0 3.5 copy-start.4
  217.2 1.9 copy-start.6
  221.2 1.0 copy-start.14
  225.7 7.2 copy-start.13
  248.5 25.3 %all-to-all-start.4 = ((f32[32,1,4096]{2,1,0:T(1,128)}), f32[32,1,4096]{2,1,0:T(1,128)}, u32[]{:S(2)}, u32[]{:S(2)}) async-start(f32[32,1,4096]{2,1,0:T(1,128)} %reshape.1277), calls=%async_computation.4 | async-start | bytes 1048576 | tf_op jit(solution)/shard_map/all_to_all | solution.py:74
  273.8 21.8 %all-to-all-start.5 = ((f32[32,1,4096]{2,1,0:T(1,128)}), f32[32,1,4096]{2,1,0:T(1,128)}, u32[]{:S(2)}, u32[]{:S(2)}) async-start(f32[32,1,4096]{2,1,0:T(1,128)} %reshape.1279), calls=%async_computation.5 | async-start | bytes 1048576 | tf_op jit(solution)/shard_map/all_to_all | solution.py:75
  303.0 2.4 copy-start.32
  320.5 5.1 copy-start.20
  325.6 3.8 copy-start.15
  325.7 3.8 copy-start.16
  337.4 1.2 copy-start.26
  338.7 1.2 copy-start.21
  361.6 24.7 %all-to-all-start.6 = ((f32[32,1,4096]{2,1,0:T(1,128)}), f32[32,1,4096]{2,1,0:T(1,128)}, u32[]{:S(2)}, u32[]{:S(2)}) async-start(f32[32,1,4096]{2,1,0:T(1,128)} %reshape.1281), calls=%async_computation.6 | async-start | bytes 1048576 | tf_op jit(solution)/shard_map/all_to_all | solution.py:74
  384.8 7.7 copy-start.37
  386.3 21.7 %all-to-all-start.7 = ((f32[32,1,4096]{2,1,0:T(1,128)}), f32[32,1,4096]{2,1,0:T(1,128)}, u32[]{:S(2)}, u32[]{:S(2)}) async-start(f32[32,1,4096]{2,1,0:T(1,128)} %reshape.1283), calls=%async_computation.7 | async-start | bytes 1048576 | tf_op jit(solution)/shard_map/all_to_all | solution.py:75
  415.3 1.2 copy-start.33
  422.4 1.0 copy-start.12
  448.1 21.3 %all-to-all-start.8 = ((f32[32,1,4096]{2,1,0:T(1,128)}), f32[32,1,4096]{2,1,0:T(1,128)S(1)}, u32[]{:S(2)}, u32[]{:S(2)}) async-start(f32[32,1,4096]{2,1,0:T(1,128)} %reshape.1285), calls=%async_computation.8 | async-start | bytes 1048576 | tf_op jit(solution)/shard_map/all_to_all | solution.py:74
  469.4 21.9 %all-to-all-start.9 = ((f32[32,1,4096]{2,1,0:T(1,128)}), f32[32,1,4096]{2,1,0:T(1,128)S(1)}, u32[]{:S(2)}, u32[]{:S(2)}) async-start(f32[32,1,4096]{2,1,0:T(1,128)} %reshape.1287), calls=%async_computation.9 | async-start | bytes 1048576 | tf_op jit(solution)/shard_map/all_to_all | solution.py:75
  495.4 1.2 copy-start.34
  507.3 1.9 copy-start.27
  527.3 1.0 copy-start.3
  528.3 2.4 copy-start.22
  533.3 7.0 copy-start.11
  555.9 25.1 %all-to-all-start.10 = ((f32[32,1,4096]{2,1,0:T(1,128)}), f32[32,1,4096]{2,1,0:T(1,128)}, u32[]{:S(2)}, u32[]{:S(2)}) async-start(f32[32,1,4096]{2,1,0:T(1,128)} %reshape.1289), calls=%async_computation.10 | async-start | bytes 1048576 | tf_op jit(solution)/shard_map/all_to_all | solution.py:74
  581.0 21.7 %all-to-all-start.11 = ((f32[32,1,4096]{2,1,0:T(1,128)}), f32[32,1,4096]{2,1,0:T(1,128)}, u32[]{:S(2)}, u32[]{:S(2)}) async-start(f32[32,1,4096]{2,1,0:T(1,128)} %reshape.1291), calls=%async_computation.11 | async-start | bytes 1048576 | tf_op jit(solution)/shard_map/all_to_all | solution.py:75
  610.0 2.4 copy-start.35
  614.1 2.1 copy-start.5
  614.1 2.1 copy-start.7
  622.7 4.2 copy-start.36
  630.6 1.0 copy-start.1
  631.6 2.4 copy-start.17
  636.6 7.2 copy-start.9
  659.4 25.1 %all-to-all-start.12 = ((f32[32,1,4096]{2,1,0:T(1,128)}), f32[32,1,4096]{2,1,0:T(1,128)}, u32[]{:S(2)}, u32[]{:S(2)}) async-start(f32[32,1,4096]{2,1,0:T(1,128)} %reshape.1293), calls=%async_computation.12 | async-start | bytes 1048576 | tf_op jit(solution)/shard_map/all_to_all | solution.py:74
  684.5 22.1 %all-to-all-start.13 = ((f32[32,1,4096]{2,1,0:T(1,128)}), f32[32,1,4096]{2,1,0:T(1,128)}, u32[]{:S(2)}, u32[]{:S(2)}) async-start(f32[32,1,4096]{2,1,0:T(1,128)} %reshape.1295), calls=%async_computation.13 | async-start | bytes 1048576 | tf_op jit(solution)/shard_map/all_to_all | solution.py:75
  713.9 2.4 copy-start.29
  731.2 5.1 copy-start.23
  751.0 1.0 copy-start
  752.0 2.4 copy-start.18
  757.0 7.0 copy-start.8
  779.8 69.1 %all-to-all-start.14 = ((f32[32,1,4096]{2,1,0:T(1,128)}), f32[32,1,4096]{2,1,0:T(1,128)}, u32[]{:S(2)}, u32[]{:S(2)}) async-start(f32[32,1,4096]{2,1,0:T(1,128)} %reshape.1297), calls=%async_computation.14 | async-start | bytes 1048576 | tf_op jit(solution)/shard_map/all_to_all | solution.py:74
  848.9 20.5 %all-to-all-start.15 = ((f32[32,1,4096]{2,1,0:T(1,128)}), f32[32,1,4096]{2,1,0:T(1,128)S(1)}, u32[]{:S(2)}, u32[]{:S(2)}) async-start(f32[32,1,4096]{2,1,0:T(1,128)} %reshape.1299), calls=%async_computation.15 | async-start | bytes 1048576 | tf_op jit(solution)/shard_map/all_to_all | solution.py:75
  873.4 1.2 copy-start.28
where the time goes:
time: 894 us; the launch traced here: 883 us
  matrix products  321 us (36%)
  other arithmetic  217 us (24%)
  local copies, waits for them, and re-layouts  176 us (20%)
  starting transfers between devices  83.1 us (9%)
  blocking collectives  40.5 us (5%)
  waiting for transfers between devices  40.4 us (5%)
    unnamed x16, other arithmetic  167 us
    dot_general x29, matrix products, complex_einsum(): imag_term = jnp.einsum(formula, left_real, table_pair[1], precision=highest)  81.2 us
    dot_general x29, matrix products, complex_einsum(): real_term = jnp.einsum(formula, left_real, table_pair[0], precision=highest)  80 us
    unnamed x115, local copies, waits for them, and re-layouts  74.6 us
    dot_general x26, matrix products, complex_einsum(): jnp.einsum(formula, left_imag, table_pair[1], precision=highest)  74.2 us
    dot_general x26, matrix products, complex_einsum(): jnp.einsum(formula, left_imag, table_pair[0], precision=highest)  73.5 us
    all_to_all x8, starting transfers between devices, regroup(): lax.all_to_all(imag_part, ('px', 'py'), split_axis=2, concat_axis=1, tile...  49.1 us
    psum x1, blocking collectives, per_device(): total = lax.psum(0.5 * jnp.sum(residual * residual), ('px', 'py'))  40.5 us
  transfers between devices with their start and end apart: 16, of which 8 were waited for; matrix products, arithmetic and copies ran while one was open for 28% of the time, Pallas kernels for 0%

commit v1 on v0

--- a/solution.py
+++ b/solution.py
@@ -6,6 +6,12 @@
 
 time_step = 0.25
 highest = lax.Precision.HIGHEST
+
+
+def trade_parts(x, name, split, join):
+    pieces = jnp.split(x, lax.axis_size(name), axis=split)
+    received = lax.all_to_all(jnp.stack(pieces), name, 0, 0)
+    return jnp.concatenate(received, axis=join)
 
 
 def factor_pair(length):
@@ -72,7 +78,7 @@
 def regroup(real_part, imag_part):
     moved_real, moved_imag = (
         lax.all_to_all(real_part, ("px", "py"), split_axis=2, concat_axis=1, tiled=True),
-        lax.all_to_all(imag_part, ("px", "py"), split_axis=2, concat_axis=1, tiled=True),
+        trade_parts(imag_part, ("px", "py"), 2, 1),
     )
     return (moved_real, moved_imag)
 

time: 894 us -> 941 us (1.053)
  local copies, waits for them, and re-layouts: 176 us -> 262 us
  other arithmetic: 217 us -> 150 us
  waiting for transfers between devices: 40.4 us -> 62.4 us
  matrix products: 321 us -> 332 us
    unnamed x115 -> x351, local copies, waits for them, and re-layouts: 74.6 us -> 166 us
    unnamed x16 -> x8, other arithmetic: 167 us -> 89.4 us
    all_to_all x8, waiting for transfers between devices: 0.02 us -> 24.3 us  [regroup(): lax.all_to_all(real_part, ('px', 'py'), split_axis=2, concat_axis=1, tile...]
    dot_general x26, matrix products: 73.5 us -> 88.7 us  [complex_einsum(): jnp.einsum(formula, left_imag, table_pair[0], precision=highest)]
    all_to_all x8 -> x0, local copies, waits for them, and re-layouts: 13.5 us -> none  [regroup(): lax.all_to_all(imag_part, ('px', 'py'), split_axis=2, concat_axis=1, tile...]
    another operation x13 -> x29, local copies, waits for them, and re-layouts: 19.6 us -> 32.5 us
    all_to_all x8, other arithmetic: 19.8 us -> 30.2 us  [trade_parts(): received = lax.all_to_all(jnp.stack(pieces), name, 0, 0)]
  transfers between devices with their start and end apart: 16 -> 16, of which waited for: 8 -> 10; matrix products, arithmetic and copies ran while one was open for 28% -> 26% of each run, Pallas kernels for 0% -> 0%
where the time goes in v1:
time: 941 us; the launch traced here: 929 us
  matrix products  332 us (35%)
  local copies, waits for them, and re-layouts  262 us (28%)
  other arithmetic  150 us (16%)
  starting transfers between devices  76 us (8%)
  waiting for transfers between devices  62.4 us (7%)
  blocking collectives  40.7 us (4%)
    unnamed x351, local copies, waits for them, and re-layouts  166 us
    unnamed x8, other arithmetic  89.4 us
    dot_general x26, matrix products, complex_einsum(): jnp.einsum(formula, left_imag, table_pair[0], precision=highest)  88.7 us
    dot_general x29, matrix products, complex_einsum(): imag_term = jnp.einsum(formula, left_real, table_pair[1], precision=highest)  79.9 us
    dot_general x29, matrix products, complex_einsum(): real_term = jnp.einsum(formula, left_real, table_pair[0], precision=highest)  76.8 us
    dot_general x26, matrix products, complex_einsum(): jnp.einsum(formula, left_imag, table_pair[1], precision=highest)  75.1 us
    all_to_all x8, starting transfers between devices, trade_parts(): received = lax.all_to_all(jnp.stack(pieces), name, 0, 0)  41.8 us
    psum x1, blocking collectives, per_device(): total = lax.psum(0.5 * jnp.sum(residual * residual), ('px', 'py'))  40.7 us
  transfers between devices with their start and end apart: 16, of which 10 were waited for; matrix products, arithmetic and copies ran while one was open for 26% of the time, Pallas kernels for 0%

profile of v1, /device:TPU:0, one launch (start us, length us, event | category | flops | bytes accessed | tf_op | source)
XLA Modules:
  0.0 929.2 jit_solution(7373497950666213398)
XLA Ops:
  13.7 10.7 %reduce = f32[2048,64]{1,0:T(8,128)S(1)} reduce(f32[2048,1,64]{2,1,0:T(1,128)} %bitcast.2155, f32[]{:T(128)} %broadcast.1623), dimensions={1}, to_apply=%bitcast.1745.reduce_sub_computation | reduce | bytes 1048580
  25.9 7.3 all-to-all-start
  43.1 5.8 all-to-all-done
  48.9 3.9 all-to-all-start.1
  59.4 8.9 all-to-all-done.1
  68.3 3.8 reduce.2
  79.3 4.2 fusion.217
  115.9 4.5 fusion.173
  120.3 3.9 fusion.43
  125.8 11.4 %reduce.3 = f32[2048,64]{1,0:T(8,128)} reduce(f32[2048,1,64]{2,1,0:T(1,128)} %bitcast.2156, f32[]{:T(128)} %broadcast.1623), dimensions={1}, to_apply=%bitcast.1747.reduce_sub_computation | reduce | bytes 1048580
  143.3 4.7 fusion.42
  171.4 6.1 all-to-all-start.3
  189.1 4.0 all-to-all-done.3
  193.0 3.8 reduce.5
  201.2 3.7 add_bitcast_fusion.12
  206.7 4.1 fusion.197
  210.9 4.2 fusion.247
  216.8 4.5 convolution_add_fusion.19
  233.1 3.9 fusion.167
  237.0 4.5 fusion.165
  246.5 11.6 %reduce.6 = f32[2048,64]{1,0:T(8,128)} reduce(f32[2048,1,64]{2,1,0:T(1,128)} %bitcast.2157, f32[]{:T(128)} %broadcast.1623), dimensions={1}, to_apply=%bitcast.1749.reduce_sub_computation | reduce | bytes 1048580
  264.1 4.7 fusion.38
  292.3 6.1 all-to-all-start.5
  314.0 3.8 reduce.8
  322.2 3.9 add_bitcast_fusion.10
  327.9 4.1 fusion.212
  332.0 4.2 fusion.242
  338.0 4.5 fusion.34
  370.8 10.6 %reduce.9 = f32[2048,64]{1,0:T(8,128)S(1)} reduce(f32[2048,1,64]{2,1,0:T(1,128)} %bitcast.2158, f32[]{:T(128)} %broadcast.1623), dimensions={1}, to_apply=%bitcast.1751.reduce_sub_computation | reduce | bytes 1048580
  382.9 5.9 all-to-all-start.6
  395.1 9.3 all-to-all-done.6
  405.2 3.7 all-to-all-start.7
  417.7 6.4 all-to-all-done.7
  424.1 3.8 reduce.11
  454.6 10.4 %reduce.12 = f32[2048,64]{1,0:T(8,128)S(1)} reduce(f32[2048,1,64]{2,1,0:T(1,128)} %bitcast.2159, f32[]{:T(128)} %broadcast.1623), dimensions={1}, to_apply=%bitcast.1753.reduce_sub_computation | reduce | bytes 1048580
  475.8 9.3 all-to-all-done.8
  485.0 3.7 all-to-all-start.9
  495.2 9.2 all-to-all-done.9
  504.4 3.8 reduce.14
  515.3 4.2 fusion.207
  552.1 4.5 fusion.141
  561.7 11.8 %reduce.15 = f32[2048,64]{1,0:T(8,128)} reduce(f32[2048,1,64]{2,1,0:T(1,128)} %bitcast.2160, f32[]{:T(128)} %broadcast.1623), dimensions={1}, to_apply=%bitcast.1755.reduce_sub_computation | reduce | bytes 1048580
  579.5 4.7 fusion.17
  607.2 6.1 all-to-all-start.11
  624.8 3.8 all-to-all-done.11
  628.7 3.8 reduce.17
  664.9 4.6 fusion.133
  674.7 11.4 %reduce.18 = f32[2048,64]{1,0:T(8,128)} reduce(f32[2048,1,64]{2,1,0:T(1,128)} %bitcast.2161, f32[]{:T(128)} %broadcast.1623), dimensions={1}, to_apply=%bitcast.1757.reduce_sub_computation | reduce | bytes 1048580
  692.1 4.7 fusion.11
  722.1 5.9 all-to-all-start.13
  728.6 40.7 %psum.7 = f32[]{:T(128)} all-reduce(f32[]{:T(128)S(6)} %mul_shard_map.3), channel_id=1, replica_groups=mesh['px'=8,'py'=4] {'px','py'}, use_global_device_ids=true, to_apply=%region_1.2 | all-reduce | flops 1 | bytes 8 | tf_op jit(solution)/shard_map/psum | solution.py:131
  782.7 3.8 reduce.20
  790.9 3.9 add_bitcast_fusion.2
  796.6 4.2 fusion.203
  800.7 4.2 fusion.225
  806.7 4.5 fusion.8
  835.6 4.5 fusion.125
  840.1 3.7 fusion.4
  845.4 11.4 %reduce.21 = f32[2048,64]{1,0:T(8,128)} reduce(f32[2048,1,64]{2,1,0:T(1,128)} %bitcast.2162, f32[]{:T(128)} %broadcast.1623), dimensions={1}, to_apply=%bitcast.1759.reduce_sub_computation | reduce | bytes 1048580
  859.5 4.8 all-to-all-start.14
  864.3 4.7 fusion.3
  892.4 6.3 all-to-all-start.15
  908.2 5.6 all-to-all-done.15
  913.8 3.8 reduce.23
  (554 shorter events, 525.4 us)
Async XLA Ops:
  25.9 23.0 %all-to-all-start = ((f32[32,1,4096]{2,1,0:T(1,128)}), f32[32,1,4096]{2,1,0:T(1,128)S(1)}, u32[]{:S(2)}, u32[]{:S(2)}) async-start(f32[32,1,4096]{2,1,0:T(1,128)} %reshape.1277), calls=%async_computation | async-start | bytes 1048576 | tf_op jit(solution)/shard_map/all_to_all | solution.py:80
  48.9 19.5 %all-to-all-start.1 = ((f32[32,1,4096]{2,1,0:T(1,128)}), f32[32,1,4096]{2,1,0:T(1,128)}, u32[]{:S(2)}, u32[]{:S(2)}) async-start(f32[32,1,4096]{2,1,0:T(1,128)} %reshape.1279), calls=%async_computation.1 | async-start | bytes 1048576 | tf_op jit(solution)/shard_map/all_to_all | solution.py:13
  86.6 1.9 copy-start.21
  106.4 1.0 copy-start.2
  107.3 2.4 copy-start.15
  139.9 31.5 %all-to-all-start.2 = ((f32[32,1,4096]{2,1,0:T(1,128)}), f32[32,1,4096]{2,1,0:T(1,128)}, u32[]{:S(2)}, u32[]{:S(2)}) async-start(f32[32,1,4096]{2,1,0:T(1,128)} %reshape.1281), calls=%async_computation.2 | async-start | bytes 1048576 | tf_op jit(solution)/shard_map/all_to_all | solution.py:80
  171.4 21.7 %all-to-all-start.3 = ((f32[32,1,4096]{2,1,0:T(1,128)}), f32[32,1,4096]{2,1,0:T(1,128)}, u32[]{:S(2)}, u32[]{:S(2)}) async-start(f32[32,1,4096]{2,1,0:T(1,128)} %reshape.1283), calls=%async_computation.3 | async-start | bytes 1048576 | tf_op jit(solution)/shard_map/all_to_all | solution.py:13
  198.3 3.0 copy-start.25
  216.8 4.5 copy-start.20
  221.3 3.5 copy-start.4
  224.5 1.9 copy-start.6
  228.5 1.0 copy-start.10
  260.8 31.5 %all-to-all-start.4 = ((f32[32,1,4096]{2,1,0:T(1,128)}), f32[32,1,4096]{2,1,0:T(1,128)}, u32[]{:S(2)}, u32[]{:S(2)}) async-start(f32[32,1,4096]{2,1,0:T(1,128)} %reshape.1285), calls=%async_computation.4 | async-start | bytes 1048576 | tf_op jit(solution)/shard_map/all_to_all | solution.py:80
  292.3 21.7 %all-to-all-start.5 = ((f32[32,1,4096]{2,1,0:T(1,128)}), f32[32,1,4096]{2,1,0:T(1,128)}, u32[]{:S(2)}, u32[]{:S(2)}) async-start(f32[32,1,4096]{2,1,0:T(1,128)} %reshape.1287), calls=%async_computation.5 | async-start | bytes 1048576 | tf_op jit(solution)/shard_map/all_to_all | solution.py:13
  319.2 3.0 copy-start.26
  338.0 5.1 copy-start.16
  343.1 3.8 copy-start.11
  343.1 3.8 copy-start.12
  354.9 1.2 copy-start.22
  356.1 1.2 copy-start.17
  382.9 21.5 %all-to-all-start.6 = ((f32[32,1,4096]{2,1,0:T(1,128)}), f32[32,1,4096]{2,1,0:T(1,128)S(1)}, u32[]{:S(2)}, u32[]{:S(2)}) async-start(f32[32,1,4096]{2,1,0:T(1,128)} %reshape.1289), calls=%async_computation.6 | async-start | bytes 1048576 | tf_op jit(solution)/shard_map/all_to_all | solution.py:80
  393.7 15.3 %copy-start.31 = (f32[1,64,2048]{2,1,0:T(8,128)S(1)}, f32[1,64,2048]{2,1,0:T(8,128)}, u32[]{:S(2)}) copy-start(f32[1,64,2048]{2,1,0:T(8,128)} %param.4) | copy-start | bytes 1572868
  404.4 0.8 copy-start.30
  405.2 18.9 %all-to-all-start.7 = ((f32[32,1,4096]{2,1,0:T(1,128)}), f32[32,1,4096]{2,1,0:T(1,128)}, u32[]{:S(2)}, u32[]{:S(2)}) async-start(f32[32,1,4096]{2,1,0:T(1,128)} %reshape.1291), calls=%async_computation.7 | async-start | bytes 1048576 | tf_op jit(solution)/shard_map/all_to_all | solution.py:13
  429.4 1.6 copy-start.27
  437.2 1.0 copy-start.8
  466.5 18.5 %all-to-all-start.8 = ((f32[32,1,4096]{2,1,0:T(1,128)}), f32[32,1,4096]{2,1,0:T(1,128)S(1)}, u32[]{:S(2)}, u32[]{:S(2)}) async-start(f32[32,1,4096]{2,1,0:T(1,128)} %reshape.1293), calls=%async_computation.8 | async-start | bytes 1048576 | tf_op jit(solution)/shard_map/all_to_all | solution.py:80
  485.0 19.3 %all-to-all-start.9 = ((f32[32,1,4096]{2,1,0:T(1,128)}), f32[32,1,4096]{2,1,0:T(1,128)}, u32[]{:S(2)}, u32[]{:S(2)}) async-start(f32[32,1,4096]{2,1,0:T(1,128)} %reshape.1295), calls=%async_computation.9 | async-start | bytes 1048576 | tf_op jit(solution)/shard_map/all_to_all | solution.py:13
  522.7 1.9 copy-start.23
  542.5 1.0 copy-start.3
  543.5 2.4 copy-start.18
  576.1 31.1 %all-to-all-start.10 = ((f32[32,1,4096]{2,1,0:T(1,128)}), f32[32,1,4096]{2,1,0:T(1,128)}, u32[]{:S(2)}, u32[]{:S(2)}) async-start(f32[32,1,4096]{2,1,0:T(1,128)} %reshape.1297), calls=%async_computation.10 | async-start | bytes 1048576 | tf_op jit(solution)/shard_map/all_to_all | solution.py:80
  607.2 21.5 %all-to-all-start.11 = ((f32[32,1,4096]{2,1,0:T(1,128)}), f32[32,1,4096]{2,1,0:T(1,128)}, u32[]{:S(2)}, u32[]{:S(2)}) async-start(f32[32,1,4096]{2,1,0:T(1,128)} %reshape.1299), calls=%async_computation.11 | async-start | bytes 1048576 | tf_op jit(solution)/shard_map/all_to_all | solution.py:13
  633.9 3.0 copy-start.28
  638.9 2.1 copy-start.5
  638.9 2.1 copy-start.7
  647.5 4.2 copy-start.29
  655.4 1.0 copy-start.1
  656.4 2.4 copy-start.13
  688.7 33.4 %all-to-all-start.12 = ((f32[32,1,4096]{2,1,0:T(1,128)}), f32[32,1,4096]{2,1,0:T(1,128)}, u32[]{:S(2)}, u32[]{:S(2)}) async-start(f32[32,1,4096]{2,1,0:T(1,128)} %reshape.1301), calls=%async_computation.12 | async-start | bytes 1048576 | tf_op jit(solution)/shard_map/all_to_all | solution.py:80
  716.8 52.6 %copy-start.9 = (f32[1,64,64,32]{1,3,2,0:T(8,128)S(1)}, f32[1,64,64,32]{1,3,2,0:T(8,128)}, u32[]{:S(2)}) copy-start(f32[1,64,64,32]{1,3,2,0:T(8,128)} %copy-done.8) | copy-start | bytes 1572868
  722.1 60.6 %all-to-all-start.13 = ((f32[32,1,4096]{2,1,0:T(1,128)}), f32[32,1,4096]{2,1,0:T(1,128)}, u32[]{:S(2)}, u32[]{:S(2)}) async-start(f32[32,1,4096]{2,1,0:T(1,128)} %reshape.1303), calls=%async_computation.13 | async-start | bytes 1048576 | tf_op jit(solution)/shard_map/all_to_all | solution.py:13
  787.9 3.0 copy-start.24
  806.7 5.1 copy-start.19
  826.1 1.0 copy-start
  827.1 2.4 copy-start.14
  859.5 32.9 %all-to-all-start.14 = ((f32[32,1,4096]{2,1,0:T(1,128)}), f32[32,1,4096]{2,1,0:T(1,128)}, u32[]{:S(2)}, u32[]{:S(2)}) async-start(f32[32,1,4096]{2,1,0:T(1,128)} %reshape.1305), calls=%async_computation.14 | async-start | bytes 1048576 | tf_op jit(solution)/shard_map/all_to_all | solution.py:80
  892.4 21.5 %all-to-all-start.15 = ((f32[32,1,4096]{2,1,0:T(1,128)}), f32[32,1,4096]{2,1,0:T(1,128)}, u32[]{:S(2)}, u32[]{:S(2)}) async-start(f32[32,1,4096]{2,1,0:T(1,128)} %reshape.1307), calls=%async_computation.15 | async-start | bytes 1048576 | tf_op jit(solution)/shard_map/all_to_all | solution.py:13
